TPU v7x, 128 devices: a whole 4x4x4 slice. The times are simulated.
128 devices in a mesh: team: 8 (over x, core), inner: 16 (over z, y).
Axes of the slice: x: 4, y: 4, z: 4, core: 2. Of those that a mesh axis runs over, the one named last changes fastest.
Arguments:
- queries: float32 [16384, 1024], P(('team', 'inner')), may hold values from -8 to 8
- passages: float32 [16384, 1024], P(('team', 'inner')), may hold values from -8 to 8
- positive: int32 [16384], P(('team', 'inner')), may hold values from 0 to 16383, as said below
Outputs:
- grad_queries: float32 [16384, 1024], P(('team', 'inner'))
- grad_passages: float32 [16384, 1024], P(('team', 'inner'))
Inputs may be any that keep to these rules, and one draw needn't show every extreme that they name: `positive`: a permutation of the passage indices 0 to 16383.
All inputs are finite; a program needn't handle non-finite values.
Results may differ from a plain program's by a relative error of at most 0.014.
Values may be sent and summed in bfloat16 or wider, within the bound.
A program may use at most 64 MiB of HBM per device.

v0:
```python
import jax
import jax.numpy as jnp
from jax import lax
from jax.sharding import Mesh
from jax.sharding import PartitionSpec as P

INNER = ("inner_0", "inner_1")
TEAM_INNER = ("team", "inner_0", "inner_1")
logit_scale_factor = 20.0
epsilon = 1e-06


def in_order(blocks, dim):
    dims = list(blocks.shape[1:])
    dims[dim] *= blocks.shape[0]
    return jnp.moveaxis(blocks, 0, dim).reshape(dims)


def sent_to_all(x, axis):
    copies = jnp.broadcast_to(x, (lax.axis_size(axis), *x.shape))
    return lax.all_to_all(copies, axis, split_axis=0, concat_axis=0, tiled=True)


def gathered_copies(x, axis, dim):
    return in_order(sent_to_all(x, axis), dim)


def taken_together(x, axis):
    everything = sent_to_all(x, axis)
    return jnp.sum(everything, axis=0)


def summed_rows(terms, axes):
    so_far = terms.astype(jnp.bfloat16)
    for axis in axes:
        so_far = lax.psum_scatter(so_far, axis, scatter_dimension=0, tiled=True)
    return so_far.astype(jnp.float32)


def split_up(x, dim, size):
    dims = x.shape
    blocks = x.reshape(*dims[:dim], size, dims[dim] // size, *dims[dim + 1 :])
    return jnp.moveaxis(blocks, dim, 0)


def summed_on_arrival(x, axis, dim):
    size = lax.axis_size(axis)
    blocks = lax.all_to_all(split_up(x, dim, size), axis, 0, 0, tiled=True)
    return jnp.sum(blocks.astype(jnp.float32), axis=0)


def unit_rows(vectors):
    length = jnp.sqrt(jnp.sum(vectors * vectors, axis=1, keepdims=True) + epsilon)
    return (vectors / length, length)


def finish(unit_vectors, length, grad_raw):
    projection = jnp.sum(unit_vectors * grad_raw, axis=1, keepdims=True)
    return (grad_raw - unit_vectors * projection) / length


def exponent(query_tile_rows, column_block):
    similarity_scores = lax.dot_general(
        query_tile_rows, column_block, (((1,), (1,)), ((), ())), preferred_element_type=jnp.float32
    )
    return jnp.exp(logit_scale_factor * similarity_scores)


def weights(query_tile_rows, column_block, target_block, row_block, column_block_total):
    exponentials = exponent(query_tile_rows, column_block)
    column_ids = lax.iota(jnp.int32, column_block.shape[0])
    is_target = (target_block[:, None] == column_ids[None, :]).astype(jnp.float32)
    combined = (
        exponentials / row_block[:, None]
        + exponentials / column_block_total[None, :]
        - 2.0 * is_target
    )
    return combined.astype(jnp.bfloat16)


def per_device(queries, passages, positive):
    shard_rows = queries.shape[0]
    feature_count = queries.shape[1]
    inner_count = lax.axis_size(INNER)
    team_count = lax.axis_size("team")
    query_unit, query_length = unit_rows(queries)
    passage_unit, passage_length = unit_rows(passages)
    query_round = query_unit.astype(jnp.bfloat16)
    passage_round = passage_unit.astype(jnp.bfloat16)
    team_queries = lax.all_gather(query_round, INNER, axis=0, tiled=True)
    team_targets = lax.all_gather(positive, INNER, axis=0, tiled=True)
    columns = gathered_copies(passage_round, "team", 0)
    team_rows = shard_rows * inner_count
    column_count = shard_rows * team_count
    owner_inner = team_targets % team_rows // shard_rows
    target_column = team_targets // team_rows * shard_rows + team_targets % shard_rows
    target_column = jnp.where(owner_inner == lax.axis_index(INNER), target_column, -1)
    block_rows = shard_rows * min(inner_count, max(1, 512 // shard_rows))
    block_count = team_rows // block_rows
    query_blocks = team_queries.reshape(block_count, block_rows, feature_count)

    def column_sums(running, query_tile_rows):
        exponentials = exponent(query_tile_rows, columns)
        return (running + jnp.sum(exponentials, axis=0), jnp.sum(exponentials, axis=1))

    column_part, row_parts = lax.scan(
        column_sums, jnp.zeros((column_count,), jnp.float32), query_blocks
    )
    row_total = taken_together(row_parts.reshape(team_rows), INNER)
    column_total = lax.psum(column_part, "team")
    query_tile_rows = team_queries
    loss_weight = weights(query_tile_rows, columns, target_column, row_total, column_total)
    query_grad = summed_rows(
        logit_scale_factor * jnp.dot(loss_weight, columns, preferred_element_type=jnp.float32),
        INNER,
    )
    loss_weight = weights(team_queries, columns, target_column, row_total, column_total)
    passage_grad = summed_on_arrival(
        (
            logit_scale_factor
            * lax.dot_general(
                loss_weight,
                team_queries,
                (((0,), (0,)), ((), ())),
                preferred_element_type=jnp.float32,
            )
        ).astype(jnp.bfloat16),
        "team",
        0,
    )
    grad_queries = finish(query_unit, query_length, query_grad)
    grad_passages = finish(passage_unit, passage_length, passage_grad)
    return (grad_queries, grad_passages)


def solution(mesh):
    finer = Mesh(mesh.devices.reshape(mesh.shape["team"], 4, 4), ("team", "inner_0", "inner_1"))
    in_specs = (P(TEAM_INNER, None), P(TEAM_INNER, None), P(TEAM_INNER))
    out_specs = (P(TEAM_INNER, None), P(TEAM_INNER, None))
    return jax.shard_map(
        per_device, mesh=finer, in_specs=in_specs, out_specs=out_specs, check_vma=False
    )
```

profile of v0, /device:TPU:0, one launch (start us, length us, event | category | flops | bytes accessed | tf_op | source)
XLA Modules:
  0.0 193.5 jit_solution(252195710733847977)
XLA Ops:
  7.2 0.0 all-gather.3.cloned.1.call-start
  7.2 1.2 multiply_reduce_fusion.2
  8.4 1.9 fusion.18
  10.2 0.0 copy-start.2
  10.2 0.0 all-gather.3.cloned.1.call-update
  10.3 1.2 multiply_reduce_fusion.1
  11.4 1.1 fusion.17
  12.6 1.6 broadcast_in_dim.16
  14.2 4.4 %all-to-all-start = ((bf16[8,128,1024]{2,1,0:T(8,128)(2,1)}), bf16[8,128,1024]{2,1,0:T(8,128)(2,1)S(1)}, u32[]{:S(2)}, u32[]{:S(2)}) async-start(bf16[8,128,1024]{2,1,0:T(8,128)(2,1)} %broadcast_in_dim.16), calls=%async_computation | async-start | bytes 4194304 | tf_op jit(solution)/shard_map/all_to_all | solution.py:21
  18.6 0.0 copy-done.2
  18.6 22.2 %all-gather = s32[16,1,128]{2,1,0:T(1,128)S(1)} all-gather(s32[1,1,128]{2,1,0:T(1,128)S(1)} %bitcast.32), channel_id=1, replica_groups=mesh['team'=8,'inner_0'=4,'inner_1'=4] {'inner_0','inner_1'}, dimensions={0}, use_global_device_ids=true | all-gather | bytes 8704 | tf_op jit(solution)/shard_map/all_gather | solution.py:91
  40.8 5.0 %all-to-all-done = bf16[8,128,1024]{2,1,0:T(8,128)(2,1)S(1)} async-done(((bf16[8,128,1024]{2,1,0:T(8,128)(2,1)}), bf16[8,128,1024]{2,1,0:T(8,128)(2,1)S(1)}, u32[]{:S(2)}, u32[]{:S(2)}) %all-to-all-start) | async-done | bytes 2097184 | tf_op jit(solution)/shard_map/all_to_all | solution.py:21
  45.8 19.0 %all-gather.3.cloned.1.call-done = bf16[2048,1024]{1,0:T(8,128)(2,1)} async-done(((bf16[128,1024]{1,0:T(8,128)(2,1)}), bf16[2048,1024]{1,0:T(8,128)(2,1)}) %all-gather.3.cloned.1.call-update) | async-done | bytes 4194320 | tf_op jit(solution)/shard_map/all_gather | solution.py:90
  64.7 11.1 %while.13 = (s32[]{:T(128)}, f32[1024]{0:T(1024)S(1)}, f32[4,512]{1,0:T(4,128)S(1)}, bf16[4,512,1024]{2,1,0:T(8,128)(2,1)}, bf16[1024,1024]{1,0:T(8,128)(2,1)S(1)}, /*index=5*/s32[]{:T(128)}, s32[]{:T(128)}) while((s32[]{:T(128)}, f32[1024]{0:T(1024)S(1)}, f32[4,512]{1,0:T(4,128)S(1)}, bf16[4,512,1024]{2,1,0:T(8,128)(2,1)}, ...), condition=%wide.region_5.6_spmd.clone, body=%wide.region_2.5_spmd.clone.sunk | while | flops 1075315200 | bytes 3168359 | solution.py:106
  64.7 2.7 %fusion.29 = (f32[512]{0:T(512)S(1)}, f32[1024]{0:T(1024)S(1)}) fusion(bf16[1024,1024]{1,0:T(8,128)(2,1)S(1)} %get-tuple-element.115, bf16[4,512,1024]{2,1,0:T(8,128)(2,1)} %get-tuple-element.114, s32[]{:T(128)S(6)} %copy.12), kind=kOutput, calls=%fused_computation.1.clone.1 | convolution fusion | flops 1075313152 | bytes 3151876 | tf_op jit(solution)/shard_map/while/body/eval_jaxpr/dot_general | solution.py:63
  67.5 0.1 dynamic_update_slice.6
  67.5 2.7 %fusion.29 = (f32[512]{0:T(512)S(1)}, f32[1024]{0:T(1024)S(1)}) fusion(bf16[1024,1024]{1,0:T(8,128)(2,1)S(1)} %get-tuple-element.115, bf16[4,512,1024]{2,1,0:T(8,128)(2,1)} %get-tuple-element.114, s32[]{:T(128)S(6)} %copy.12), kind=kOutput, calls=%fused_computation.1.clone.1 | convolution fusion | flops 1075313152 | bytes 3151876 | tf_op jit(solution)/shard_map/while/body/eval_jaxpr/dot_general | solution.py:63
  70.2 0.1 dynamic_update_slice.6
  70.3 2.7 %fusion.29 = (f32[512]{0:T(512)S(1)}, f32[1024]{0:T(1024)S(1)}) fusion(bf16[1024,1024]{1,0:T(8,128)(2,1)S(1)} %get-tuple-element.115, bf16[4,512,1024]{2,1,0:T(8,128)(2,1)} %get-tuple-element.114, s32[]{:T(128)S(6)} %copy.12), kind=kOutput, calls=%fused_computation.1.clone.1 | convolution fusion | flops 1075313152 | bytes 3151876 | tf_op jit(solution)/shard_map/while/body/eval_jaxpr/dot_general | solution.py:63
  73.0 0.1 dynamic_update_slice.6
  73.1 2.7 %fusion.29 = (f32[512]{0:T(512)S(1)}, f32[1024]{0:T(1024)S(1)}) fusion(bf16[1024,1024]{1,0:T(8,128)(2,1)S(1)} %get-tuple-element.115, bf16[4,512,1024]{2,1,0:T(8,128)(2,1)} %get-tuple-element.114, s32[]{:T(128)S(6)} %copy.12), kind=kOutput, calls=%fused_computation.1.clone.1 | convolution fusion | flops 1075313152 | bytes 3151876 | tf_op jit(solution)/shard_map/while/body/eval_jaxpr/dot_general | solution.py:63
  75.8 0.1 dynamic_update_slice.6
  75.9 0.7 broadcast_in_dim.36
  76.6 5.3 %all-to-all-start.1 = ((f32[16,1,2048]{2,1,0:T(1,128)}), f32[16,1,2048]{2,1,0:T(1,128)S(1)}, u32[]{:S(2)}, u32[]{:S(2)}) async-start(f32[16,1,2048]{2,1,0:T(1,128)} %broadcast_in_dim.36), calls=%async_computation.1 | async-start | bytes 262144 | tf_op jit(solution)/shard_map/all_to_all | solution.py:21
  81.9 0.0 reduce-scatter.3.cloned.1.call-start
  82.0 14.4 %psum.7 = f32[1024]{0:T(1024)S(1)} all-reduce(f32[1024]{0:T(1024)S(1)} %get-tuple-element.31), channel_id=1, replica_groups=mesh['team'=8,'inner_0'=4,'inner_1'=4] {'team'}, use_global_device_ids=true, to_apply=%region_7.8 | all-reduce | flops 1024 | bytes 8192 | tf_op jit(solution)/shard_map/psum | solution.py:110
  96.4 0.0 all-to-all-done.1
  96.4 0.1 reduce_sum.74
  96.5 7.9 %subtract_convert_fusion = bf16[2048,1024]{1,0:T(8,128)(2,1)S(1)} fusion(bf16[2048,1024]{1,0:T(8,128)(2,1)} %bitcast.34, bf16[1024,1024]{1,0:T(8,128)(2,1)S(1)} %get-tuple-element.125, s32[2048]{0:T(1024)S(1)} %fusion.12, f32[1024]{0:T(1024)S(1)} %psum.7, f32[2048]{0:T(1024)S(1)} %reduce_sum.74), kind=kOutput, calls=%fused_computation.9 | convolution fusion | flops 4311744512 | bytes 10506240 | tf_op jit(solution)/shard_map/dot_general | solution.py:63
  104.4 0.0 copy-start.3
  104.4 2.0 %copy-done.3 = bf16[2048,1024]{1,0:T(8,128)(2,1)} copy-done((bf16[2048,1024]{1,0:T(8,128)(2,1)}, bf16[2048,1024]{1,0:T(8,128)(2,1)S(1)}, u32[]{:S(2)}) %copy-start.3) | copy-done | bytes 4194328
  106.4 6.1 %multiply_convert_fusion = bf16[2048,1024]{1,0:T(8,128)(2,1)} fusion(bf16[2048,1024]{1,0:T(8,128)(2,1)S(1)} %subtract_convert_fusion, bf16[1024,1024]{1,0:T(8,128)(2,1)S(1)} %get-tuple-element.125), kind=kOutput, calls=%fused_computation.8 | convolution fusion | flops 4299161600 | bytes 10485760 | tf_op jit(solution)/shard_map/dot_general | solution.py:114
  112.5 0.0 reduce-scatter.3.cloned.1.call-update
  112.5 9.4 %multiply_convert_fusion.1 = bf16[1024,1024]{1,0:T(8,128)(2,1)} fusion(bf16[2048,1024]{1,0:T(8,128)(2,1)} %copy-done.3, bf16[2048,1024]{1,0:T(8,128)(2,1)} %bitcast.35), kind=kOutput, calls=%fused_computation.12 | convolution fusion | flops 4297064448 | bytes 10485760 | tf_op jit(solution)/shard_map/dot_general | solution.py:121
  121.9 3.7 %all-to-all-start.2 = ((bf16[8,128,1024]{2,1,0:T(8,128)(2,1)}), bf16[8,128,1024]{2,1,0:T(8,128)(2,1)S(1)}, u32[]{:S(2)}, u32[]{:S(2)}) async-start(bf16[8,128,1024]{2,1,0:T(8,128)(2,1)} %bitcast.27), calls=%async_computation.4 | async-start | bytes 4194304 | tf_op jit(solution)/shard_map/all_to_all | solution.py:48
  125.6 0.0 copy-start.1
  125.6 0.0 reduce-scatter.5.cloned.1.call-start
  125.7 32.5 %reduce-scatter.3.cloned.1.call-done = bf16[512,1024]{1,0:T(8,128)(2,1)} async-done(((bf16[2048,1024]{1,0:T(8,128)(2,1)}), bf16[512,1024]{1,0:T(8,128)(2,1)}) %reduce-scatter.3.cloned.1.call-update) | async-done | bytes 1048592 | tf_op jit(solution)/shard_map/reduce_scatter | solution.py:36
  158.2 0.0 reduce-scatter.5.cloned.1.call-update
  158.2 0.0 all-to-all-done.2
  158.2 0.4 convert_reduce_fusion
  158.6 0.0 copy-done
  158.6 0.2 multiply_reduce_fusion
  158.8 1.0 subtract_divide_fusion
  159.8 24.1 %reduce-scatter.5.cloned.1.call-done = bf16[128,1024]{1,0:T(8,128)(2,1)} async-done(((bf16[512,1024]{1,0:T(8,128)(2,1)}), bf16[128,1024]{1,0:T(8,128)(2,1)}) %reduce-scatter.5.cloned.1.call-update) | async-done | bytes 262160 | tf_op jit(solution)/shard_map/reduce_scatter | solution.py:36
  183.9 0.0 copy-done.1
  183.9 1.2 fusion.6
  185.1 1.9 fusion.7
  (11 shorter events, 0.1 us)
Async XLA Ops:
  7.2 57.6 %all-gather.3.cloned.1.call-start = ((), (), s32[]{:S(2)}) async-start(), calls=%async_computation.5 | async-start | bytes 4456448 | tf_op jit(solution)/shard_map/all_gather | solution.py:90
  10.2 8.4 %copy-start.2 = (s32[128]{0:T(128)S(1)}, s32[128]{0:T(128)}, u32[]{:S(2)}) copy-start(s32[128]{0:T(128)} %param.7) | copy-start | bytes 1540
  14.2 31.6 %all-to-all-start = ((bf16[8,128,1024]{2,1,0:T(8,128)(2,1)}), bf16[8,128,1024]{2,1,0:T(8,128)(2,1)S(1)}, u32[]{:S(2)}, u32[]{:S(2)}) async-start(bf16[8,128,1024]{2,1,0:T(8,128)(2,1)} %broadcast_in_dim.16), calls=%async_computation | async-start | bytes 4194304 | tf_op jit(solution)/shard_map/all_to_all | solution.py:21
  76.6 19.8 %all-to-all-start.1 = ((f32[16,1,2048]{2,1,0:T(1,128)}), f32[16,1,2048]{2,1,0:T(1,128)S(1)}, u32[]{:S(2)}, u32[]{:S(2)}) async-start(f32[16,1,2048]{2,1,0:T(1,128)} %broadcast_in_dim.36), calls=%async_computation.1 | async-start | bytes 262144 | tf_op jit(solution)/shard_map/all_to_all | solution.py:21
  81.9 76.3 %reduce-scatter.3.cloned.1.call-start = ((), (), s32[]{:S(2)}) async-start(), calls=%async_computation.6 | async-start | bytes 5242880 | tf_op jit(solution)/shard_map/reduce_scatter | solution.py:36
  104.4 2.0 %copy-start.3 = (bf16[2048,1024]{1,0:T(8,128)(2,1)}, bf16[2048,1024]{1,0:T(8,128)(2,1)S(1)}, u32[]{:S(2)}) copy-start(bf16[2048,1024]{1,0:T(8,128)(2,1)S(1)} %subtract_convert_fusion) | copy-start | bytes 12582916
  121.9 36.7 %copy-start = (f32[128,1024]{1,0:T(8,128)S(1)}, f32[128,1024]{1,0:T(8,128)}, u32[]{:S(2)}) copy-start(f32[128,1024]{1,0:T(8,128)} %param.6) | copy-start | bytes 1572868
  121.9 36.3 %all-to-all-start.2 = ((bf16[8,128,1024]{2,1,0:T(8,128)(2,1)}), bf16[8,128,1024]{2,1,0:T(8,128)(2,1)S(1)}, u32[]{:S(2)}, u32[]{:S(2)}) async-start(bf16[8,128,1024]{2,1,0:T(8,128)(2,1)} %bitcast.27), calls=%async_computation.4 | async-start | bytes 4194304 | tf_op jit(solution)/shard_map/all_to_all | solution.py:48
  125.6 58.3 %copy-start.1 = (f32[128,1024]{1,0:T(8,128)S(1)}, f32[128,1024]{1,0:T(8,128)}, u32[]{:S(2)}) copy-start(f32[128,1024]{1,0:T(8,128)} %param.5) | copy-start | bytes 1572868
  125.6 58.3 %reduce-scatter.5.cloned.1.call-start = ((), (), s32[]{:S(2)}) async-start(), calls=%async_computation.7 | async-start | bytes 1310720 | tf_op jit(solution)/shard_map/reduce_scatter | solution.py:36
Sparse Core Ops, SparseCore 0:
  10.7 54.0 all-gather.2
  112.6 45.5 reduce-scatter.2
  160.6 23.2 reduce-scatter.4
where the time goes:
time: 194 us
  waiting for transfers between devices  80.6 us (42%)
  blocking collectives  36.5 us (19%)
  matrix products  34.2 us (18%)
  between operations  13.9 us (7%)
  starting transfers between devices  13.6 us (7%)
  other arithmetic  10.1 us (5%)
  local copies, waits for them, and re-layouts  4.51 us (2%)
    reduce_scatter x2, waiting for transfers between devices, summed_rows(): so_far = lax.psum_scatter(so_far, axis, scatter_dimension=0, tiled=True)  56.6 us
    all_gather x1, blocking collectives, per_device(): team_targets = lax.all_gather(positive, INNER, axis=0, tiled=True)  22.2 us
    all_gather x1, waiting for transfers between devices, per_device(): team_queries = lax.all_gather(query_round, INNER, axis=0, tiled=True)  19 us
    dot_general x5, matrix products, exponent(): lax.dot_general(query_tile_rows, column_block, (((1,), (1,)), ((), ())),...  18.8 us
    psum x1, blocking collectives, per_device(): column_total = lax.psum(column_part, 'team')  14.4 us
    all_to_all x2, starting transfers between devices, sent_to_all(): return lax.all_to_all(copies, axis, split_axis=0, concat_axis=0, tiled=True)  9.7 us
    dot_general x1, matrix products, per_device(): lax.dot_general(loss_weight, team_queries, (((0,), (0,)), ((), ())), pref...  9.41 us
    dot_general x1, matrix products, per_device(): jnp.dot(loss_weight, columns, preferred_element_type=jnp.float32)  6.06 us
  transfers between devices with their start and end apart: 6, of which 4 were waited for; matrix products, arithmetic and copies ran while one was open for 8% of the time, Pallas kernels for 0%

commit v1 on v0

--- a/solution.py
+++ b/solution.py
@@ -107,7 +107,10 @@
         column_sums, jnp.zeros((column_count,), jnp.float32), query_blocks
     )
     row_total = taken_together(row_parts.reshape(team_rows), INNER)
-    column_total = lax.psum(column_part, "team")
+    count, column_total = (lax.axis_size("team"), column_part)
+    for hop in [1 << k for k in range(count.bit_length() - 1)]:
+        swap = [(i, i ^ hop) for i in range(count)]
+        column_total = column_total + lax.ppermute(column_total, "team", swap)
     query_tile_rows = team_queries
     loss_weight = weights(query_tile_rows, columns, target_column, row_total, column_total)
     query_grad = summed_rows(

time: 194 us -> 212 us (1.093)
  waiting for transfers between devices: 80.6 us -> 109 us
  blocking collectives: 36.5 us -> 20 us
  starting transfers between devices: 13.6 us -> 18.7 us
  matrix products: 34.2 us -> 37.6 us
    all_to_all x2, waiting for transfers between devices: 5 us -> 29.7 us  [sent_to_all(): return lax.all_to_all(copies, axis, split_axis=0, concat_axis=0, tiled=True)]
    psum x1 -> x0, blocking collectives: 14.4 us -> none  [per_device(): column_total = lax.psum(column_part, 'team')]
    ppermute x0 -> x3, starting transfers between devices: none -> 4.49 us  [per_device(): column_total = column_total + lax.ppermute(column_total, 'team', swap)]
    ppermute x0 -> x3, waiting for transfers between devices: none -> 3.56 us  [per_device(): column_total = column_total + lax.ppermute(column_total, 'team', swap)]
    dot_general x1, matrix products: 6.06 us -> 8.29 us  [per_device(): jnp.dot(loss_weight, columns, preferred_element_type=jnp.float32)]
  transfers between devices with their start and end apart: 6 -> 9, of which waited for: 4 -> 7; matrix products, arithmetic and copies ran while one was open for 8% -> 7% of each run, Pallas kernels for 0% -> 0%
where the time goes in v1:
time: 212 us
  waiting for transfers between devices  109 us (51%)
  matrix products  37.6 us (18%)
  blocking collectives  20 us (9%)
  starting transfers between devices  18.7 us (9%)
  between operations  13.8 us (7%)
  other arithmetic  10.1 us (5%)
  local copies, waits for them, and re-layouts  2.54 us (1%)
    reduce_scatter x2, waiting for transfers between devices, summed_rows(): so_far = lax.psum_scatter(so_far, axis, scatter_dimension=0, tiled=True)  56.5 us
    all_to_all x2, waiting for transfers between devices, sent_to_all(): return lax.all_to_all(copies, axis, split_axis=0, concat_axis=0, tiled=True)  29.7 us
    all_gather x1, blocking collectives, per_device(): team_targets = lax.all_gather(positive, INNER, axis=0, tiled=True)  20 us
    dot_general x5, matrix products, exponent(): lax.dot_general(query_tile_rows, column_block, (((1,), (1,)), ((), ())),...  19.9 us
    all_gather x1, waiting for transfers between devices, per_device(): team_queries = lax.all_gather(query_round, INNER, axis=0, tiled=True)  19 us
    all_to_all x2, starting transfers between devices, sent_to_all(): return lax.all_to_all(copies, axis, split_axis=0, concat_axis=0, tiled=True)  9.98 us
    dot_general x1, matrix products, per_device(): lax.dot_general(loss_weight, team_queries, (((0,), (0,)), ((), ())), pref...  9.41 us
    dot_general x1, matrix products, per_device(): jnp.dot(loss_weight, columns, preferred_element_type=jnp.float32)  8.29 us
  transfers between devices with their start and end apart: 9, of which 7 were waited for; matrix products, arithmetic and copies ran while one was open for 7% of the time, Pallas kernels for 0%

profile of v1, /device:TPU:0, one launch (start us, length us, event | category | flops | bytes accessed | tf_op | source)
XLA Modules:
  0.0 211.7 jit_solution(12258316440650528211)
XLA Ops:
  7.2 0.0 all-gather.3.cloned.1.call-start
  7.2 1.2 multiply_reduce_fusion.2
  8.4 1.9 fusion.18
  10.2 0.0 all-gather.3.cloned.1.call-update
  10.3 1.2 multiply_reduce_fusion.1
  11.4 1.1 fusion.17
  12.6 1.6 broadcast_in_dim.16
  14.2 4.4 %all-to-all-start = ((bf16[8,128,1024]{2,1,0:T(8,128)(2,1)}), bf16[8,128,1024]{2,1,0:T(8,128)(2,1)S(1)}, u32[]{:S(2)}, u32[]{:S(2)}) async-start(bf16[8,128,1024]{2,1,0:T(8,128)(2,1)} %broadcast_in_dim.16), calls=%async_computation | async-start | bytes 4194304 | tf_op jit(solution)/shard_map/all_to_all | solution.py:21
  18.6 27.2 %all-to-all-done = bf16[8,128,1024]{2,1,0:T(8,128)(2,1)S(1)} async-done(((bf16[8,128,1024]{2,1,0:T(8,128)(2,1)}), bf16[8,128,1024]{2,1,0:T(8,128)(2,1)S(1)}, u32[]{:S(2)}, u32[]{:S(2)}) %all-to-all-start) | async-done | bytes 2097184 | tf_op jit(solution)/shard_map/all_to_all | solution.py:21
  45.8 19.0 %all-gather.3.cloned.1.call-done = bf16[2048,1024]{1,0:T(8,128)(2,1)} async-done(((bf16[128,1024]{1,0:T(8,128)(2,1)}), bf16[2048,1024]{1,0:T(8,128)(2,1)}) %all-gather.3.cloned.1.call-update) | async-done | bytes 4194320 | tf_op jit(solution)/shard_map/all_gather | solution.py:90
  64.7 10.9 %while.13 = (s32[]{:T(128)}, f32[1024]{0:T(1024)S(1)}, f32[4,512]{1,0:T(4,128)S(1)}, bf16[4,512,1024]{2,1,0:T(8,128)(2,1)}, bf16[1024,1024]{1,0:T(8,128)(2,1)S(1)}, /*index=5*/s32[]{:T(128)}, s32[]{:T(128)}) while((s32[]{:T(128)}, f32[1024]{0:T(1024)S(1)}, f32[4,512]{1,0:T(4,128)S(1)}, bf16[4,512,1024]{2,1,0:T(8,128)(2,1)}, ...), condition=%wide.region_5.6_spmd.clone, body=%wide.region_2.5_spmd.clone.sunk | while | flops 1075315200 | bytes 3168359 | solution.py:106
  64.7 2.7 %fusion.29 = (f32[512]{0:T(512)S(1)}, f32[1024]{0:T(1024)S(1)}) fusion(bf16[1024,1024]{1,0:T(8,128)(2,1)S(1)} %get-tuple-element.115, bf16[4,512,1024]{2,1,0:T(8,128)(2,1)} %get-tuple-element.114, s32[]{:T(128)S(6)} %copy.12), kind=kOutput, calls=%fused_computation.1.clone.1 | convolution fusion | flops 1075313152 | bytes 3151876 | tf_op jit(solution)/shard_map/while/body/eval_jaxpr/dot_general | solution.py:63
  67.4 0.1 dynamic_update_slice.6
  67.5 2.7 %fusion.29 = (f32[512]{0:T(512)S(1)}, f32[1024]{0:T(1024)S(1)}) fusion(bf16[1024,1024]{1,0:T(8,128)(2,1)S(1)} %get-tuple-element.115, bf16[4,512,1024]{2,1,0:T(8,128)(2,1)} %get-tuple-element.114, s32[]{:T(128)S(6)} %copy.12), kind=kOutput, calls=%fused_computation.1.clone.1 | convolution fusion | flops 1075313152 | bytes 3151876 | tf_op jit(solution)/shard_map/while/body/eval_jaxpr/dot_general | solution.py:63
  70.1 0.1 dynamic_update_slice.6
  70.2 2.7 %fusion.29 = (f32[512]{0:T(512)S(1)}, f32[1024]{0:T(1024)S(1)}) fusion(bf16[1024,1024]{1,0:T(8,128)(2,1)S(1)} %get-tuple-element.115, bf16[4,512,1024]{2,1,0:T(8,128)(2,1)} %get-tuple-element.114, s32[]{:T(128)S(6)} %copy.12), kind=kOutput, calls=%fused_computation.1.clone.1 | convolution fusion | flops 1075313152 | bytes 3151876 | tf_op jit(solution)/shard_map/while/body/eval_jaxpr/dot_general | solution.py:63
  72.9 0.1 dynamic_update_slice.6
  72.9 2.7 %fusion.29 = (f32[512]{0:T(512)S(1)}, f32[1024]{0:T(1024)S(1)}) fusion(bf16[1024,1024]{1,0:T(8,128)(2,1)S(1)} %get-tuple-element.115, bf16[4,512,1024]{2,1,0:T(8,128)(2,1)} %get-tuple-element.114, s32[]{:T(128)S(6)} %copy.12), kind=kOutput, calls=%fused_computation.1.clone.1 | convolution fusion | flops 1075313152 | bytes 3151876 | tf_op jit(solution)/shard_map/while/body/eval_jaxpr/dot_general | solution.py:63
  75.6 0.1 dynamic_update_slice.6
  75.7 0.1 collective-permute-start
  75.8 1.2 collective-permute-done
  76.9 1.5 collective-permute-start.1
  78.4 0.0 copy-done.2
  78.4 20.0 %all-gather = s32[16,1,128]{2,1,0:T(1,128)S(1)} all-gather(s32[1,1,128]{2,1,0:T(1,128)S(1)} %bitcast.32), channel_id=1, replica_groups=mesh['team'=8,'inner_0'=4,'inner_1'=4] {'inner_0','inner_1'}, dimensions={0}, use_global_device_ids=true | all-gather | bytes 8704 | tf_op jit(solution)/shard_map/all_gather | solution.py:91
  98.4 0.7 broadcast_in_dim.36
  99.2 5.6 %all-to-all-start.1 = ((f32[16,1,2048]{2,1,0:T(1,128)}), f32[16,1,2048]{2,1,0:T(1,128)S(1)}, u32[]{:S(2)}, u32[]{:S(2)}) async-start(f32[16,1,2048]{2,1,0:T(1,128)} %broadcast_in_dim.36), calls=%async_computation.1 | async-start | bytes 262144 | tf_op jit(solution)/shard_map/all_to_all | solution.py:21
  104.7 0.0 reduce-scatter.3.cloned.1.call-start
  104.8 0.0 collective-permute-done.1
  104.8 2.9 %collective-permute-start.2 = (f32[1024]{0:T(1024)S(1)}, f32[1024]{0:T(1024)S(1)}, u32[]{:S(2)}, u32[]{:S(2)}) collective-permute-start(f32[1024]{0:T(1024)S(1)} %add.60), channel_id=1, source_target_pairs={{0,64},{16,80},{32,96},{48,112},{64,0},{80,16},{96,32},{112,48},{1... | collective-permute-start | bytes 12296 | tf_op jit(solution)/shard_map/ppermute | solution.py:113
  107.8 2.4 %collective-permute-done.2 = f32[1024]{0:T(1024)S(1)} collective-permute-done((f32[1024]{0:T(1024)S(1)}, f32[1024]{0:T(1024)S(1)}, u32[]{:S(2)}, u32[]{:S(2)}) %collective-permute-start.2) | collective-permute-done | bytes 4128 | tf_op jit(solution)/shard_map/ppermute | solution.py:113
  110.2 2.5 %all-to-all-done.1 = f32[16,1,2048]{2,1,0:T(1,128)S(1)} async-done(((f32[16,1,2048]{2,1,0:T(1,128)}), f32[16,1,2048]{2,1,0:T(1,128)S(1)}, u32[]{:S(2)}, u32[]{:S(2)}) %all-to-all-start.1) | async-done | bytes 131104 | tf_op jit(solution)/shard_map/all_to_all | solution.py:21
  112.7 0.1 reduce_sum.74
  112.8 9.3 %subtract_convert_fusion = bf16[2048,1024]{1,0:T(8,128)(2,1)} fusion(s32[2048]{0:T(1024)S(1)} %fusion.12, f32[1024]{0:T(1024)S(1)} %add.61, f32[2048]{0:T(1024)S(1)} %reduce_sum.74, bf16[2048,1024]{1,0:T(8,128)(2,1)} %bitcast.34, bf16[1024,1024]{1,0:T(8,128)(2,1)S(1)} %get-tuple-element.125), kind=kOutput, calls=%fused_computation.9 | convolution fusion | flops 4311744512 | bytes 10506240 | tf_op jit(solution)/shard_map/dot_general | solution.py:63
  122.1 8.3 %multiply_convert_fusion = bf16[2048,1024]{1,0:T(8,128)(2,1)} fusion(bf16[2048,1024]{1,0:T(8,128)(2,1)} %subtract_convert_fusion, bf16[1024,1024]{1,0:T(8,128)(2,1)S(1)} %get-tuple-element.125), kind=kOutput, calls=%fused_computation.8 | convolution fusion | flops 4299161600 | bytes 10485760 | tf_op jit(solution)/shard_map/dot_general | solution.py:117
  130.4 0.0 reduce-scatter.3.cloned.1.call-update
  130.4 9.4 %multiply_convert_fusion.1 = bf16[1024,1024]{1,0:T(8,128)(2,1)} fusion(bf16[2048,1024]{1,0:T(8,128)(2,1)} %subtract_convert_fusion, bf16[2048,1024]{1,0:T(8,128)(2,1)} %bitcast.35), kind=kOutput, calls=%fused_computation.12 | convolution fusion | flops 4297064448 | bytes 10485760 | tf_op jit(solution)/shard_map/dot_general | solution.py:124
  139.8 4.1 %all-to-all-start.2 = ((bf16[8,128,1024]{2,1,0:T(8,128)(2,1)}), bf16[8,128,1024]{2,1,0:T(8,128)(2,1)S(1)}, u32[]{:S(2)}, u32[]{:S(2)}) async-start(bf16[8,128,1024]{2,1,0:T(8,128)(2,1)} %bitcast.27), calls=%async_computation.4 | async-start | bytes 4194304 | tf_op jit(solution)/shard_map/all_to_all | solution.py:48
  143.9 0.0 reduce-scatter.5.cloned.1.call-start
  143.9 32.3 %reduce-scatter.3.cloned.1.call-done = bf16[512,1024]{1,0:T(8,128)(2,1)} async-done(((bf16[2048,1024]{1,0:T(8,128)(2,1)}), bf16[512,1024]{1,0:T(8,128)(2,1)}) %reduce-scatter.3.cloned.1.call-update) | async-done | bytes 1048592 | tf_op jit(solution)/shard_map/reduce_scatter | solution.py:36
  176.3 0.0 reduce-scatter.5.cloned.1.call-update
  176.3 0.0 all-to-all-done.2
  176.3 0.3 convert_reduce_fusion
  176.7 0.0 copy-done
  176.7 0.2 multiply_reduce_fusion
  176.9 1.0 subtract_divide_fusion
  177.9 24.2 %reduce-scatter.5.cloned.1.call-done = bf16[128,1024]{1,0:T(8,128)(2,1)} async-done(((bf16[512,1024]{1,0:T(8,128)(2,1)}), bf16[128,1024]{1,0:T(8,128)(2,1)}) %reduce-scatter.5.cloned.1.call-update) | async-done | bytes 262160 | tf_op jit(solution)/shard_map/reduce_scatter | solution.py:36
  202.1 1.2 fusion.6
  203.3 1.9 fusion.7
  (17 shorter events, 0.1 us)
Async XLA Ops:
  7.2 57.6 %all-gather.3.cloned.1.call-start = ((), (), s32[]{:S(2)}) async-start(), calls=%async_computation.5 | async-start | bytes 4456448 | tf_op jit(solution)/shard_map/all_gather | solution.py:90
  14.2 31.6 %all-to-all-start = ((bf16[8,128,1024]{2,1,0:T(8,128)(2,1)}), bf16[8,128,1024]{2,1,0:T(8,128)(2,1)S(1)}, u32[]{:S(2)}, u32[]{:S(2)}) async-start(bf16[8,128,1024]{2,1,0:T(8,128)(2,1)} %broadcast_in_dim.16), calls=%async_computation | async-start | bytes 4194304 | tf_op jit(solution)/shard_map/all_to_all | solution.py:21
  64.7 13.7 %copy-start.2 = (s32[128]{0:T(128)S(1)}, s32[128]{0:T(128)}, u32[]{:S(2)}) copy-start(s32[128]{0:T(128)} %param.7) | copy-start | bytes 1540
  75.7 1.2 collective-permute-start
  76.9 27.9 %collective-permute-start.1 = (f32[1024]{0:T(1024)S(1)}, f32[1024]{0:T(1024)S(1)}, u32[]{:S(2)}, u32[]{:S(2)}) collective-permute-start(f32[1024]{0:T(1024)S(1)} %add.59), channel_id=1, source_target_pairs={{0,32},{16,48},{32,0},{48,16},{64,96},{80,112},{96,64},{112,80},{1... | collective-permute-start | bytes 12296 | tf_op jit(solution)/shard_map/ppermute | solution.py:113
  99.2 13.6 %all-to-all-start.1 = ((f32[16,1,2048]{2,1,0:T(1,128)}), f32[16,1,2048]{2,1,0:T(1,128)S(1)}, u32[]{:S(2)}, u32[]{:S(2)}) async-start(f32[16,1,2048]{2,1,0:T(1,128)} %broadcast_in_dim.36), calls=%async_computation.1 | async-start | bytes 262144 | tf_op jit(solution)/shard_map/all_to_all | solution.py:21
  104.7 71.5 %reduce-scatter.3.cloned.1.call-start = ((), (), s32[]{:S(2)}) async-start(), calls=%async_computation.6 | async-start | bytes 5242880 | tf_op jit(solution)/shard_map/reduce_scatter | solution.py:36
  104.8 5.4 %collective-permute-start.2 = (f32[1024]{0:T(1024)S(1)}, f32[1024]{0:T(1024)S(1)}, u32[]{:S(2)}, u32[]{:S(2)}) collective-permute-start(f32[1024]{0:T(1024)S(1)} %add.60), channel_id=1, source_target_pairs={{0,64},{16,80},{32,96},{48,112},{64,0},{80,16},{96,32},{112,48},{1... | collective-permute-start | bytes 12296 | tf_op jit(solution)/shard_map/ppermute | solution.py:113
  139.8 36.9 %copy-start = (f32[128,1024]{1,0:T(8,128)S(1)}, f32[128,1024]{1,0:T(8,128)}, u32[]{:S(2)}) copy-start(f32[128,1024]{1,0:T(8,128)} %param.6) | copy-start | bytes 1572868
  139.8 36.5 %all-to-all-start.2 = ((bf16[8,128,1024]{2,1,0:T(8,128)(2,1)}), bf16[8,128,1024]{2,1,0:T(8,128)(2,1)S(1)}, u32[]{:S(2)}, u32[]{:S(2)}) async-start(bf16[8,128,1024]{2,1,0:T(8,128)(2,1)} %bitcast.27), calls=%async_computation.4 | async-start | bytes 4194304 | tf_op jit(solution)/shard_map/all_to_all | solution.py:48
  143.9 58.2 %copy-start.1 = (f32[128,1024]{1,0:T(8,128)S(1)}, f32[128,1024]{1,0:T(8,128)}, u32[]{:S(2)}) copy-start(f32[128,1024]{1,0:T(8,128)} %param.5) | copy-start | bytes 1572868
  143.9 58.2 %reduce-scatter.5.cloned.1.call-start = ((), (), s32[]{:S(2)}) async-start(), calls=%async_computation.7 | async-start | bytes 1310720 | tf_op jit(solution)/shard_map/reduce_scatter | solution.py:36
Sparse Core Ops, SparseCore 0:
  10.7 53.9 all-gather.2
  130.5 45.7 reduce-scatter.2
  178.7 23.3 reduce-scatter.4
